TPU v7x, 32 devices: a whole 2x2x4 slice. The times are simulated.
32 devices in a mesh: ens: 4 (over y, x), slab: 8 (over z, core).
Axes of the slice: x: 2, y: 2, z: 4, core: 2. Of those that a mesh axis runs over, the one named last changes fastest.
Arguments:
- velocity: float32 [4, 3, 8, 2048, 1024], P('ens', None, None, 'slab'), may hold values from -6 to 6
- cutoffs: int32 [4, 2, 8], P('ens'), may hold values from 128 to 511, as said below
- plane_index: int32 [4], P('ens'), may hold values from 0 to 2047
- boundary_index: int32 [4], P('ens'), may hold values from 0 to 2047
Outputs:
- blended: float32 [4, 3, 8, 2048, 1024], P('ens', None, None, 'slab')
Inputs may be any that keep to these rules, and one draw needn't show every extreme that they name: `cutoffs`: row 0 lies in 256 to 511 and row 1 in 128 to 255; in every member some level has row 0 equal to 511 and some level has row 1 equal to 255.
All inputs are finite; a program needn't handle non-finite values.
Results may differ from a plain program's by a relative error of at most 0.0003.
Values sent between devices are 32-bit elements; how exact they have to be, the bound alone decides.
A program may use at most 128 MiB of HBM per device.

v0:
```python
import math
import jax
import jax.numpy as jnp
from jax import lax
from jax.sharding import PartitionSpec as P

KX = 512
KY = 256
highest = lax.Precision.HIGHEST


def spread(value, axis, source):
    kept = jnp.where(lax.axis_index(axis) == source, value, 0).astype(value.dtype)
    return lax.psum(kept, axis)


def shifted(block, axis, distance):
    devices = range(lax.axis_size(axis))
    route = [((i - distance) % len(devices), i) for i in devices]
    return lax.ppermute(block, axis, route)


def basis_pair(length, mode_count):
    position = jnp.arange(length, dtype=jnp.int32)
    wavenum = jnp.arange(mode_count, dtype=jnp.int32)
    angles = (position[:, None] * wavenum[None, :] % length).astype(jnp.float32) * (
        2.0 * math.pi / length
    )
    basis_cols = jnp.concatenate([jnp.cos(angles), jnp.sin(angles)], axis=1)
    weight = jnp.where(wavenum == 0, 1.0, 2.0).astype(jnp.float32) / length
    weight = jnp.concatenate([weight, weight])
    return (basis_cols * weight[None, :], basis_cols.T)


def mode_keep(levels_cut, mode_count):
    wavenum = jnp.tile(jnp.arange(mode_count, dtype=jnp.int32), 2)
    return (wavenum[None, :] <= levels_cut[:, None]).astype(jnp.float32)


def x_filter(columns, analysis_x, synthesis_x, keep_x):
    coeffs = (
        jnp.einsum("xk,czxj->czkj", analysis_x, columns, precision=highest)
        * keep_x[None, :, :, None]
    )
    return jnp.einsum("kx,czkj->czxj", synthesis_x, coeffs, precision=highest)


def on_device(velocity, cutoffs, plane_index, boundary_index):
    devices = lax.axis_size("slab")
    member_rows = velocity.shape[3]
    across = velocity.shape[4]
    along = member_rows * devices
    analysis_x, synthesis_x = basis_pair(along, KX)
    analysis_y, synthesis_y = basis_pair(across, KY)
    keep_x = mode_keep(cutoffs[0, 0], KX)
    keep_y = mode_keep(cutoffs[0, 1], KY)
    own_field = velocity[0]
    spectra = (
        jnp.einsum("czxy,yj->czxj", own_field, analysis_y, precision=highest)
        * keep_y[None, :, None, :]
    )
    columns = lax.all_to_all(spectra, "slab", split_axis=3, concat_axis=2, tiled=True)
    smooth = x_filter(columns, analysis_x, synthesis_x, keep_x)
    returned = lax.all_to_all(smooth, "slab", split_axis=2, concat_axis=3, tiled=True)
    result = jnp.einsum("czxj,jy->czxy", returned, synthesis_y, precision=highest)
    first_row = lax.axis_index("slab") * member_rows
    local_index = jnp.clip(plane_index[0] - first_row, 0, member_rows - 1)
    plane_part = lax.dynamic_index_in_dim(result, local_index, 2, keepdims=False)
    source_plane = spread(plane_part, "slab", plane_index[0] // member_rows)
    inflow = shifted(source_plane, "ens", 1)
    streamwise = first_row + jnp.arange(member_rows, dtype=jnp.int32)
    offset = jnp.abs(streamwise - boundary_index[0])
    distance = jnp.minimum(offset, along - offset)
    relax = jnp.exp(-distance.astype(jnp.float32) / (along / 4.0))
    weight = relax[None, None, :, None]
    blended = result + weight * (inflow[:, :, None, :] - result)
    return blended[None]


def solution(mesh):
    in_specs = (P("ens", None, None, "slab", None), P("ens", None, None), P("ens"), P("ens"))
    out_specs = P("ens", None, None, "slab", None)
    return jax.shard_map(
        on_device, mesh=mesh, in_specs=in_specs, out_specs=out_specs, check_vma=False
    )
```

profile of v0, /device:TPU:8, one launch (start us, length us, event | category | flops | bytes accessed | tf_op | source)
XLA Modules:
  0.0 1089.4 jit_solution(2496585179114449928)
XLA Ops:
  6.5 4.1 fusion.37
  10.7 0.8 slice_bitcast_fusion
  11.5 84.5 %bitcast_multiply_fusion = f32[3,8,256,512]{2,3,1,0:T(8,128)} fusion(f32[8,512]{1,0:T(8,128)S(1)} %compare_convert_fusion.1, f32[1,3,8,256,1024]{4,3,2,1,0:T(8,128)} %param.4, f32[1024,256]{1,0:T(8,128)S(1)} %get-tuple-element.7, f32[1024,256]{1,0:T(8,128)S(1)} %get-tuple-element.8, f32[512]{0:T(512)S(1)} %pad_maximum_fusion.7), kind=kOutput, calls=%fused_computation.3 | convolution fusion | flops 38658899968 | bytes 39864320 | tf_op jit(solution)/shard_map/czxy,yj->czxj/dot_general | solution.py:59
  96.0 16.3 %copy.17 = f32[3,8,256,512]{2,1,0,3:T(8,128)} copy(f32[3,8,256,512]{2,3,1,0:T(8,128)} %bitcast_multiply_fusion) | data formatting | bytes 25165824 | tf_op jit(solution)/shard_map/mul | solution.py:59
  112.3 5.5 all-to-all-start
  118.0 17.5 %fusion.27 = (f32[2048,512]{1,0:T(8,128)}, f32[2048,512]{1,0:T(8,128)}) fusion(), kind=kLoop, calls=%fused_computation.29 | loop fusion | flops 14680064 | bytes 8388608 | tf_op jit(solution)/shard_map/sin | solution.py:29
  135.6 252.6 %all-to-all-done = f32[3,8,256,512]{2,1,0,3:T(8,128)} async-done(((f32[3,8,256,512]{2,1,0,3:T(8,128)}), f32[3,8,256,512]{2,1,0,3:T(8,128)}, u32[]{:S(2)}, u32[]{:S(2)}) %all-to-all-start) | async-done | bytes 12582944 | tf_op jit(solution)/shard_map/all_to_all | solution.py:62
  388.1 16.6 %copy.36 = f32[3,8,256,8,64]{2,3,4,1,0:T(8,128)} copy(f32[3,8,256,8,64]{2,1,0,4,3:T(8,128)} %bitcast.4) | data formatting | bytes 25165824 | tf_op jit(solution)/shard_map/all_to_all | solution.py:62
  404.8 13.6 %all_to_all.29 = f32[3,8,2048,64]{2,3,1,0:T(8,128)} reshape(f32[3,8,8,256,64]{3,2,4,1,0:T(8,128)} %bitcast.77) | data formatting | bytes 25165824 | tf_op jit(solution)/shard_map/all_to_all | solution.py:62
  418.4 47.2 %fusion.4 = f32[3,8,64,1024]{3,2,1,0:T(8,128)} fusion(f32[3,8,2048,64]{2,3,1,0:T(8,128)} %all_to_all.29, f32[2048,512]{1,0:T(8,128)} %get-tuple-element.9, f32[2048,512]{1,0:T(8,128)} %get-tuple-element.10, f32[1024]{0:T(1024)S(1)} %pad_maximum_fusion.6), kind=kOutput, calls=%fused_computation.8 | convolution fusion | flops 38658899968 | bytes 27267072 | tf_op jit(solution)/shard_map/xk,czxj->czkj/dot_general | solution.py:42
  465.6 44.3 %fusion.9 = f32[3,8,2048,64]{2,3,1,0:T(8,128)} fusion(f32[2048,512]{1,0:T(8,128)S(1)} %copy-done.1, f32[2048,512]{1,0:T(8,128)S(1)} %copy-done.2, f32[3,8,64,1024]{3,2,1,0:T(8,128)} %fusion.4, f32[8,1024]{1,0:T(8,128)S(1)} %compare_convert_fusion), kind=kOutput, calls=%fused_computation.16 | convolution fusion | flops 38658375680 | bytes 27295744 | tf_op jit(solution)/shard_map/kx,czkj->czxj/dot_general | solution.py:45
  509.9 17.7 %copy.19 = f32[3,8,2048,64]{3,1,0,2:T(8,128)} copy(f32[3,8,2048,64]{2,3,1,0:T(8,128)} %fusion.9) | data formatting | bytes 25165824 | tf_op jit(solution)/shard_map/kx,czkj->czxj/transpose | solution.py:45
  527.6 20.5 %reshape.91 = f32[8,1,393216]{2,1,0:T(1,128)} reshape(f32[2048,3,8,64]{3,2,1,0:T(8,128)} %bitcast.74) | data formatting | bytes 25165824
  548.1 8.8 all-to-all-start.1
  557.6 269.6 %all-to-all-done.1 = f32[8,1,393216]{2,1,0:T(1,128)} async-done(((f32[8,1,393216]{2,1,0:T(1,128)}), f32[8,1,393216]{2,1,0:T(1,128)}, u32[]{:S(2)}, u32[]{:S(2)}) %all-to-all-start.1) | async-done | bytes 12582944 | tf_op jit(solution)/shard_map/all_to_all | solution.py:64
  827.7 36.8 %reduce = f32[8,393216]{1,0:T(8,128)} reduce(f32[8,1,393216]{2,1,0:T(1,128)} %all-to-all-done.1, f32[]{:T(128)} %broadcast.88), dimensions={1}, to_apply=%all_to_all.30.reduce_sub_computation | reduce | bytes 25165828 | tf_op jit(solution)/shard_map/all_to_all | solution.py:64
  864.5 23.2 %reshape.92 = f32[2048,3,8,64]{3,2,1,0:T(8,128)} reshape(f32[8,393216]{1,0:T(8,128)} %reduce) | data formatting | bytes 25165824
  887.7 18.7 %copy.21 = f32[3,8,256,8,64]{2,4,3,1,0:T(8,128)} copy(f32[3,8,256,8,64]{4,1,0,2,3:T(8,128)} %bitcast.75) | data formatting | bytes 25165824 | tf_op jit(solution)/shard_map/all_to_all | solution.py:64
  906.4 85.2 %fusion.24 = f32[3,8,256,1024]{3,2,1,0:T(8,128)S(1)} fusion(f32[3,8,256,512]{2,3,1,0:T(8,128)} %bitcast.76, f32[1024,256]{1,0:T(8,128)S(1)} %get-tuple-element.7, f32[1024,256]{1,0:T(8,128)S(1)} %get-tuple-element.8), kind=kOutput, calls=%fused_computation.26 | convolution fusion | flops 38655229952 | bytes 39845888 | tf_op jit(solution)/shard_map/czxj,jy->czxy/dot_general | solution.py:65
  991.6 8.9 copy-done
  1001.9 55.8 %all-reduce.2.cloned.1.call-done = f32[3,8,1024]{2,1,0:T(8,128)} async-done(((f32[3,8,1024]{2,1,0:T(8,128)}), f32[3,8,1024]{2,1,0:T(8,128)}) %all-reduce.2.cloned.1.call-update) | async-done | bytes 98320 | tf_op jit(solution)/shard_map/psum | solution.py:14
  1057.7 1.5 collective-permute-start
  1059.2 4.2 collective-permute-done
  1063.4 18.8 %add_bitcast_fusion = f32[1,3,8,256,1024]{4,3,2,1,0:T(8,128)} fusion(f32[3,8,256,1024]{3,2,1,0:T(8,128)} %copy-done, f32[3,8,1024]{2,1,0:T(8,128)S(1)} %collective-permute-done, f32[256]{0:T(256)S(1)} %fusion.42), kind=kLoop, calls=%fused_computation.2 | loop fusion | flops 18874368 | bytes 50430976 | tf_op jit(solution)/shard_map/broadcast_in_dim | solution.py:77
  (21 shorter events, 1.5 us)
Async XLA Ops:
  112.3 275.8 %all-to-all-start = ((f32[3,8,256,512]{2,1,0,3:T(8,128)}), f32[3,8,256,512]{2,1,0,3:T(8,128)}, u32[]{:S(2)}, u32[]{:S(2)}) async-start(f32[3,8,256,512]{2,1,0,3:T(8,128)} %copy.17), calls=%async_computation | async-start | bytes 25165824 | tf_op jit(solution)/shard_map/all_to_all | solution.py:62
  418.4 47.2 %copy-start.1 = (f32[2048,512]{1,0:T(8,128)S(1)}, f32[2048,512]{1,0:T(8,128)}, u32[]{:S(2)}) copy-start(f32[2048,512]{1,0:T(8,128)} %get-tuple-element.9) | copy-start | bytes 12582916
  418.4 47.2 %copy-start.2 = (f32[2048,512]{1,0:T(8,128)S(1)}, f32[2048,512]{1,0:T(8,128)}, u32[]{:S(2)}) copy-start(f32[2048,512]{1,0:T(8,128)} %get-tuple-element.10) | copy-start | bytes 12582916
  548.1 279.1 %all-to-all-start.1 = ((f32[8,1,393216]{2,1,0:T(1,128)}), f32[8,1,393216]{2,1,0:T(1,128)}, u32[]{:S(2)}, u32[]{:S(2)}) async-start(f32[8,1,393216]{2,1,0:T(1,128)} %reshape.91), calls=%async_computation.1 | async-start | bytes 25165824 | tf_op jit(solution)/shard_map/all_to_all | solution.py:64
  556.9 500.8 %all-reduce.2.cloned.1.call-start = ((), (), s32[]{:S(2)}) async-start(), calls=%async_computation.2 | async-start | bytes 196608 | tf_op jit(solution)/shard_map/psum | solution.py:14
  991.5 8.9 copy-start
  1057.7 5.7 collective-permute-start
Sparse Core Ops, SparseCore 0:
  1001.4 56.2 all-reduce.1
where the time goes:
time: 1090 us
  waiting for transfers between devices  582 us (53%)
  matrix products  261 us (24%)
  local copies, waits for them, and re-layouts  138 us (13%)
  other arithmetic  77.5 us (7%)
  starting transfers between devices  15.8 us (1%)
  between operations  15.2 us (1%)
    all_to_all x1, waiting for transfers between devices, on_device(): lax.all_to_all(smooth, 'slab', split_axis=2, concat_axis=3, tiled=True)  270 us
    all_to_all x1, waiting for transfers between devices, on_device(): lax.all_to_all(spectra, 'slab', split_axis=3, concat_axis=2, tiled=True)  253 us
    dot_general x1, matrix products, on_device(): jnp.einsum('czxj,jy->czxy', returned, synthesis_y, precision=highest)  85.2 us
    dot_general x1, matrix products, on_device(): jnp.einsum('czxy,yj->czxj', own_field, analysis_y, precision=highest)  84.5 us
    psum x1, waiting for transfers between devices, spread(): return lax.psum(kept, axis)  55.8 us
    unnamed x13, local copies, waits for them, and re-layouts  53.3 us
    dot_general x1, matrix products, x_filter(): jnp.einsum('xk,czxj->czkj', analysis_x, columns, precision=highest)  47.2 us
    dot_general x1, matrix products, x_filter(): return jnp.einsum('kx,czkj->czxj', synthesis_x, coeffs, precision=highest)  44.3 us
  transfers between devices with their start and end apart: 4, of which 4 were waited for; matrix products, arithmetic and copies ran while one was open for 2% of the time, Pallas kernels for 0%

commit v1 on v0

--- a/solution.py
+++ b/solution.py
@@ -9,9 +9,15 @@
 highest = lax.Precision.HIGHEST
 
 
+def add_all(x, mesh_axis):
+    parts = lax.all_gather(x, mesh_axis, axis=0, tiled=False)
+    result = parts.sum(axis=0)
+    return result
+
+
 def spread(value, axis, source):
     kept = jnp.where(lax.axis_index(axis) == source, value, 0).astype(value.dtype)
-    return lax.psum(kept, axis)
+    return add_all(kept, axis)
 
 
 def shifted(block, axis, distance):

time: 1090 us -> 1060 us (0.972)
  waiting for transfers between devices: 582 us -> 526 us
  blocking collectives: 0 us -> 16.4 us
  matrix products: 261 us -> 275 us
  between operations: 15.2 us -> 1.62 us
    psum x1 -> x0, waiting for transfers between devices: 55.8 us -> none  [spread(): return lax.psum(kept, axis)]
    all_gather x0 -> x1, blocking collectives: none -> 16.4 us  [add_all(): parts = lax.all_gather(x, mesh_axis, axis=0, tiled=False)]
    dot_general x1, matrix products: 85.2 us -> 99.6 us  [on_device(): jnp.einsum('czxj,jy->czxy', returned, synthesis_y, precision=highest)]
    unnamed x13 -> x12, local copies, waits for them, and re-layouts: 53.3 us -> 52.7 us
  transfers between devices with their start and end apart: 4 -> 3, of which waited for: 4 -> 3; matrix products, arithmetic and copies ran while one was open for 2% -> 2% of each run, Pallas kernels for 0% -> 0%
where the time goes in v1:
time: 1060 us; the launch traced here: 1050 us
  waiting for transfers between devices  526 us (50%)
  matrix products  275 us (26%)
  local copies, waits for them, and re-layouts  137 us (13%)
  other arithmetic  77.3 us (7%)
  blocking collectives  16.4 us (2%)
  starting transfers between devices  16.2 us (2%)
    all_to_all x1, waiting for transfers between devices, on_device(): lax.all_to_all(smooth, 'slab', split_axis=2, concat_axis=3, tiled=True)  269 us
    all_to_all x1, waiting for transfers between devices, on_device(): lax.all_to_all(spectra, 'slab', split_axis=3, concat_axis=2, tiled=True)  253 us
    dot_general x1, matrix products, on_device(): jnp.einsum('czxj,jy->czxy', returned, synthesis_y, precision=highest)  99.6 us
    dot_general x1, matrix products, on_device(): jnp.einsum('czxy,yj->czxj', own_field, analysis_y, precision=highest)  84.4 us
    unnamed x12, local copies, waits for them, and re-layouts  52.7 us
    dot_general x1, matrix products, x_filter(): jnp.einsum('xk,czxj->czkj', analysis_x, columns, precision=highest)  47.2 us
    dot_general x1, matrix products, x_filter(): return jnp.einsum('kx,czkj->czxj', synthesis_x, coeffs, precision=highest)  44.3 us
    all_to_all x1, other arithmetic, on_device(): lax.all_to_all(smooth, 'slab', split_axis=2, concat_axis=3, tiled=True)  36.6 us
  transfers between devices with their start and end apart: 3, of which 3 were waited for; matrix products, arithmetic and copies ran while one was open for 2% of the time, Pallas kernels for 0%

profile of v1, /device:TPU:8, one launch (start us, length us, event | category | flops | bytes accessed | tf_op | source)
XLA Modules:
  0.0 1049.9 jit_solution(16726689763349839345)
XLA Ops:
  0.0 4.1 fusion.37
  4.1 0.8 slice_bitcast_fusion
  5.0 84.4 %bitcast_multiply_fusion = f32[3,8,256,512]{2,3,1,0:T(8,128)} fusion(f32[8,512]{1,0:T(8,128)S(1)} %compare_convert_fusion.1, f32[1,3,8,256,1024]{4,3,2,1,0:T(8,128)} %param.4, f32[1024,256]{1,0:T(8,128)S(1)} %get-tuple-element.7, f32[1024,256]{1,0:T(8,128)S(1)} %get-tuple-element.8, f32[512]{0:T(512)S(1)} %pad_maximum_fusion.7), kind=kOutput, calls=%fused_computation.3 | convolution fusion | flops 38658899968 | bytes 39864320 | tf_op jit(solution)/shard_map/czxy,yj->czxj/dot_general | solution.py:65
  89.4 16.3 %copy.18 = f32[3,8,256,512]{2,1,0,3:T(8,128)} copy(f32[3,8,256,512]{2,3,1,0:T(8,128)} %bitcast_multiply_fusion) | data formatting | bytes 25165824 | tf_op jit(solution)/shard_map/mul | solution.py:65
  105.7 5.5 all-to-all-start
  111.4 17.5 %fusion.27 = (f32[2048,512]{1,0:T(8,128)}, f32[2048,512]{1,0:T(8,128)}) fusion(), kind=kLoop, calls=%fused_computation.29 | loop fusion | flops 14680064 | bytes 8388608 | tf_op jit(solution)/shard_map/sin | solution.py:35
  128.9 252.6 %all-to-all-done = f32[3,8,256,512]{2,1,0,3:T(8,128)} async-done(((f32[3,8,256,512]{2,1,0,3:T(8,128)}), f32[3,8,256,512]{2,1,0,3:T(8,128)}, u32[]{:S(2)}, u32[]{:S(2)}) %all-to-all-start) | async-done | bytes 12582944 | tf_op jit(solution)/shard_map/all_to_all | solution.py:68
  381.5 16.6 %copy.36 = f32[3,8,256,8,64]{2,3,4,1,0:T(8,128)} copy(f32[3,8,256,8,64]{2,1,0,4,3:T(8,128)} %bitcast.4) | data formatting | bytes 25165824 | tf_op jit(solution)/shard_map/all_to_all | solution.py:68
  398.1 13.6 %all_to_all.29 = f32[3,8,2048,64]{2,3,1,0:T(8,128)} reshape(f32[3,8,8,256,64]{3,2,4,1,0:T(8,128)} %bitcast.75) | data formatting | bytes 25165824 | tf_op jit(solution)/shard_map/all_to_all | solution.py:68
  411.8 47.2 %fusion.4 = f32[3,8,64,1024]{3,2,1,0:T(8,128)} fusion(f32[3,8,2048,64]{2,3,1,0:T(8,128)} %all_to_all.29, f32[2048,512]{1,0:T(8,128)} %get-tuple-element.9, f32[2048,512]{1,0:T(8,128)} %get-tuple-element.10, f32[1024]{0:T(1024)S(1)} %pad_maximum_fusion.6), kind=kOutput, calls=%fused_computation.8 | convolution fusion | flops 38658899968 | bytes 27267072 | tf_op jit(solution)/shard_map/xk,czxj->czkj/dot_general | solution.py:48
  459.0 44.3 %fusion.9 = f32[3,8,2048,64]{2,3,1,0:T(8,128)} fusion(f32[2048,512]{1,0:T(8,128)S(1)} %copy-done.1, f32[2048,512]{1,0:T(8,128)S(1)} %copy-done.2, f32[3,8,64,1024]{3,2,1,0:T(8,128)} %fusion.4, f32[8,1024]{1,0:T(8,128)S(1)} %compare_convert_fusion), kind=kOutput, calls=%fused_computation.16 | convolution fusion | flops 38658375680 | bytes 27295744 | tf_op jit(solution)/shard_map/kx,czkj->czxj/dot_general | solution.py:51
  503.2 17.9 %copy.20 = f32[3,8,2048,64]{3,1,0,2:T(8,128)} copy(f32[3,8,2048,64]{2,3,1,0:T(8,128)} %fusion.9) | data formatting | bytes 25165824 | tf_op jit(solution)/shard_map/kx,czkj->czxj/transpose | solution.py:51
  521.2 20.5 %reshape.102 = f32[8,1,393216]{2,1,0:T(1,128)} reshape(f32[2048,3,8,64]{3,2,1,0:T(8,128)} %bitcast.72) | data formatting | bytes 25165824
  541.6 8.8 all-to-all-start.1
  551.7 269.0 %all-to-all-done.1 = f32[8,1,393216]{2,1,0:T(1,128)} async-done(((f32[8,1,393216]{2,1,0:T(1,128)}), f32[8,1,393216]{2,1,0:T(1,128)}, u32[]{:S(2)}, u32[]{:S(2)}) %all-to-all-start.1) | async-done | bytes 12582944 | tf_op jit(solution)/shard_map/all_to_all | solution.py:70
  821.2 36.6 %reduce = f32[8,393216]{1,0:T(8,128)} reduce(f32[8,1,393216]{2,1,0:T(1,128)} %all-to-all-done.1, f32[]{:T(128)} %broadcast.102), dimensions={1}, to_apply=%all_to_all.30.reduce_sub_computation | reduce | bytes 25165828 | tf_op jit(solution)/shard_map/all_to_all | solution.py:70
  857.8 23.2 %reshape.103 = f32[2048,3,8,64]{3,2,1,0:T(8,128)} reshape(f32[8,393216]{1,0:T(8,128)} %reduce) | data formatting | bytes 25165824
  881.1 18.6 %copy.22 = f32[3,8,256,8,64]{2,4,3,1,0:T(8,128)} copy(f32[3,8,256,8,64]{4,1,0,2,3:T(8,128)} %bitcast.73) | data formatting | bytes 25165824 | tf_op jit(solution)/shard_map/all_to_all | solution.py:70
  899.7 99.6 %fusion.24 = f32[3,8,256,1024]{3,2,1,0:T(8,128)S(1)} fusion(f32[3,8,256,512]{2,3,1,0:T(8,128)} %bitcast.74, f32[1024,256]{1,0:T(8,128)S(1)} %get-tuple-element.7, f32[1024,256]{1,0:T(8,128)S(1)} %get-tuple-element.8), kind=kOutput, calls=%fused_computation.26 | convolution fusion | flops 38655229952 | bytes 39845888 | tf_op jit(solution)/shard_map/czxj,jy->czxy/dot_general | solution.py:71
  999.3 8.9 copy-done
  1008.3 16.4 %all-gather = f32[24,8,1,1024]{3,1,2,0:T(8,128)S(1)} all-gather(f32[3,8,1,1024]{3,1,2,0:T(8,128)S(1)} %copy.24), channel_id=2, replica_groups=mesh['ens'=4,'slab'=8] {'slab'}, dimensions={0}, use_global_device_ids=true | all-gather | bytes 884736 | tf_op jit(solution)/shard_map/all_gather | solution.py:13
  1024.7 1.9 collective-permute-start
  1026.7 4.2 collective-permute-done
  1030.9 18.8 %add_bitcast_fusion = f32[1,3,8,256,1024]{4,3,2,1,0:T(8,128)} fusion(f32[3,8,256,1024]{3,2,1,0:T(8,128)} %copy-done, f32[3,8,1024]{2,1,0:T(8,128)S(1)} %collective-permute-done, f32[256]{0:T(256)S(1)} %fusion.42), kind=kLoop, calls=%fused_computation.2 | loop fusion | flops 18874368 | bytes 50430976 | tf_op jit(solution)/shard_map/broadcast_in_dim | solution.py:83
  (20 shorter events, 0.9 us)
Async XLA Ops:
  105.7 275.8 %all-to-all-start = ((f32[3,8,256,512]{2,1,0,3:T(8,128)}), f32[3,8,256,512]{2,1,0,3:T(8,128)}, u32[]{:S(2)}, u32[]{:S(2)}) async-start(f32[3,8,256,512]{2,1,0,3:T(8,128)} %copy.18), calls=%async_computation | async-start | bytes 25165824 | tf_op jit(solution)/shard_map/all_to_all | solution.py:68
  411.8 47.2 %copy-start.1 = (f32[2048,512]{1,0:T(8,128)S(1)}, f32[2048,512]{1,0:T(8,128)}, u32[]{:S(2)}) copy-start(f32[2048,512]{1,0:T(8,128)} %get-tuple-element.9) | copy-start | bytes 12582916
  411.8 47.2 %copy-start.2 = (f32[2048,512]{1,0:T(8,128)S(1)}, f32[2048,512]{1,0:T(8,128)}, u32[]{:S(2)}) copy-start(f32[2048,512]{1,0:T(8,128)} %get-tuple-element.10) | copy-start | bytes 12582916
  541.6 279.1 %all-to-all-start.1 = ((f32[8,1,393216]{2,1,0:T(1,128)}), f32[8,1,393216]{2,1,0:T(1,128)}, u32[]{:S(2)}, u32[]{:S(2)}) async-start(f32[8,1,393216]{2,1,0:T(1,128)} %reshape.102), calls=%async_computation.1 | async-start | bytes 25165824 | tf_op jit(solution)/shard_map/all_to_all | solution.py:70
  999.3 8.9 copy-start
  1024.7 6.2 collective-permute-start
